TPU v7x, 32 devices: a whole 2x2x4 slice. The times are simulated.
32 devices in a mesh: tm: 4 (over y, x), space: 8 (over z, core).
Axes of the slice: x: 2, y: 2, z: 4, core: 2. Of those that a mesh axis runs over, the one named last changes fastest.
Arguments:
- queries: bfloat16 [4096, 4096], P(('tm', 'space')), may hold values from -20 to 20
- key_vectors: bfloat16 [4096, 4096], P(('tm', 'space')), may hold values from -20 to 20
- value_vectors: bfloat16 [4096, 4096], P(('tm', 'space')), may hold values from -6 to 6
- out_weight: bfloat16 [4096, 6144], P(None, 'space'), may hold values from -0.375 to 0.375
- frame_mask: int32 [4, 4], replicated, may hold values 0 or 1
Outputs:
- projected: bfloat16 [4096, 6144], P('tm', 'space')
All inputs are finite; a program needn't handle non-finite values.
Results may differ from a plain program's by a relative error of at most 0.0075.
Values may be sent and summed in bfloat16 or wider, within the bound.
A program may use at most 128 MiB of HBM per device.

v0:
```python
import functools
import math

import jax
import jax.numpy as jnp
from jax import lax
from jax.experimental import pallas as pl
from jax.experimental.pallas import tpu as pltpu
from jax.sharding import PartitionSpec as P

HD = 128
MESH = pl.DeviceIdType.MESH


def kernel(
    frames, places, heads,
    q_hbm, k_hbm, v_hbm, w_hbm, mask_ref, out_ref,
    qb, kvb, kvx, kvy, gat, wv, acc,
    a_send, a_recv, x_send, x_recv, y_send, y_recv,
    g_send, g_recv, p_recv, w_sem,
):
    f = lax.axis_index("tm")
    s = lax.axis_index("space")
    tok = q_hbm.shape[0]
    rows = tok * places
    half = rows // 2
    chips = places // 2
    z = lax.div(s, 2)
    core = lax.rem(s, 2)
    odd = lax.rem(f, 2)
    partner = f + 1 - 2 * odd
    onward = lax.rem(f + 2 - 4 * odd + frames, frames)
    behind = lax.rem(f - 2 + 4 * odd + frames, frames)
    far = lax.rem(f - 1 + 2 * odd + frames, frames)
    mate = 2 * z + 1 - core

    barrier = pltpu.get_barrier_semaphore()

    def greet(j, carry):
        pl.semaphore_signal(
            barrier, inc=1, device_id=(f, lax.rem(s + j, places)), device_id_type=MESH
        )
        return carry

    lax.fori_loop(1, places, greet, 0)
    for other in (partner, onward, behind):
        pl.semaphore_signal(barrier, inc=1, device_id=(other, s), device_id_type=MESH)
    pl.semaphore_wait(barrier, places - 1 + 3)

    def remote(src, dst, send, recv, tm_to, space_to):
        return pltpu.make_async_remote_copy(
            src_ref=src, dst_ref=dst, send_sem=send, recv_sem=recv,
            device_id=(tm_to, space_to), device_id_type=MESH,
        )

    def landing(t, h):
        return qb.at[h] if t == 2 else kvb.at[t, h]

    sources = (k_hbm, v_hbm, q_hbm)

    def send_head(h):
        for t in range(3):
            mine = landing(t, h).at[pl.ds(pl.multiple_of(s * tok, tok), tok), :]

            def one(j, carry):
                to = lax.rem(s + j, places)
                cols = pl.ds(pl.multiple_of((to * heads + h) * HD, HD), HD)
                remote(
                    sources[t].at[:, cols], mine, a_send.at[h, t], a_recv.at[h, t], f, to
                ).start()
                return carry

            lax.fori_loop(1, places, one, 0)
            cols = pl.ds(pl.multiple_of((s * heads + h) * HD, HD), HD)
            pltpu.make_async_copy(sources[t].at[:, cols], mine, a_recv.at[h, t]).start()

    def whole_wait(ref, sem):
        pltpu.make_async_copy(ref, ref, sem).wait()

    def x_copy(h, t):
        return remote(
            kvb.at[t, h], kvx.at[t, h], x_send.at[h, t], x_recv.at[h, t], partner, s
        )

    def y_copy(h, t):
        return remote(
            kvx.at[t, h], kvy.at[t, h], y_send.at[h, t], y_recv.at[h, t], onward, s
        )

    def columns(place):
        return pl.ds(pl.multiple_of(place * HD, HD), HD)

    def g_copy(g, place, slot, recv, to):
        part = gat.at[g // 2, pl.ds(g % 2 * half, half), columns(place)]
        return remote(part, part, g_send.at[g, slot], recv, f, to)

    def own_copies(g):
        return [
            (z < chips - 1, g_copy(g, s, 0, g_recv.at[g, 0, 0], s + 2)),
            (z > 0, g_copy(g, s, 1, g_recv.at[g, 1, 0], s - 2)),
            (None, g_copy(g, s, 2, p_recv.at[g, z], mate)),
        ]

    def relay_copies(g, k):
        low, high = s - 2 * k, s + 2 * k
        base = 3 + 4 * (k - 1)
        copies = []
        if k < chips - 1:
            copies.append(((z >= k) & (z < chips - 1),
                           lambda: g_copy(g, low, base, g_recv.at[g, 0, k], s + 2)))
        copies.append((z >= k, lambda: g_copy(g, low, base + 1, p_recv.at[g, z - k], mate)))
        if k < chips - 1:
            copies.append(((z + k <= chips - 1) & (z > 0),
                           lambda: g_copy(g, high, base + 2, g_recv.at[g, 1, k], s - 2)))
        copies.append((z + k <= chips - 1,
                       lambda: g_copy(g, high, base + 3, p_recv.at[g, z + k], mate)))
        return copies

    def start_own(g):
        for cond, copy in own_copies(g):
            if cond is None:
                copy.start()
            else:
                pl.when(cond)(copy.start)

    def relay(g, k):
        @pl.when(z >= k)
        def _():
            g_copy(g, s - 2 * k, 0, g_recv.at[g, 0, k - 1], mate).wait_recv()

        @pl.when(z + k <= chips - 1)
        def _():
            g_copy(g, s + 2 * k, 0, g_recv.at[g, 1, k - 1], mate).wait_recv()

        for cond, make in relay_copies(g, k):
            @pl.when(cond)
            def _():
                make().start()

    near_pen = jnp.where(mask_ref[f, partner] == 1, 0.0, jnp.inf).astype(jnp.float32)
    far_pen = jnp.where(mask_ref[f, far] == 1, 0.0, jnp.inf).astype(jnp.float32)
    factor = math.log2(math.e) / math.sqrt(HD)
    q_tile = min(256, half)
    tiles = rows // q_tile

    def attend(h, first, last):
        def tile(i, carry):
            at = pl.ds(pl.multiple_of(i * q_tile, q_tile), q_tile)
            q = qb[h, at, :]
            places_kv = ((kvb, None), (kvx, near_pen), (kvy, far_pen))
            scores = []
            top = None
            for ref, pen in places_kv:
                sc = lax.dot_general(
                    q, ref[0, h], (((1,), (1,)), ((), ())),
                    preferred_element_type=jnp.float32,
                )
                scores.append(sc)
                best = jnp.max(sc, axis=1, keepdims=True)
                best = best if pen is None else best - pen
                top = best if top is None else jnp.maximum(top, best)
            total = None
            mixed = None
            for sc, (ref, pen) in zip(scores, places_kv):
                level = top if pen is None else top + pen
                e = jnp.exp2((sc - level) * factor)
                part = jnp.sum(e, axis=1, keepdims=True)
                prod = jnp.dot(
                    e.astype(jnp.bfloat16), ref[1, h], preferred_element_type=jnp.float32
                )
                total = part if total is None else total + part
                mixed = prod if mixed is None else mixed + prod
            gat[h, at, columns(s)] = (mixed / total).astype(jnp.bfloat16)
            return carry

        lax.fori_loop(first, last, tile, 0)

    p_tile = min(256, half)

    def project(c):
        g = c // 2
        for o in range(chips):
            g_copy(c, 2 * o + 1 - core, 0, p_recv.at[c, o], mate).wait_recv()
        if c % 2 == 0:
            whole_wait(wv.at[g], w_sem.at[g])

        def tile(i, carry):
            at = pl.ds(pl.multiple_of(c % 2 * half + i * p_tile, p_tile), p_tile)
            prod = jnp.dot(gat[g, at, :], wv[g], preferred_element_type=jnp.float32)
            if g > 0:
                prod = prod + acc[at, :]
            if g == heads - 1:
                out_ref[at, :] = prod.astype(out_ref.dtype)
            else:
                acc[at, :] = prod
            return carry

        lax.fori_loop(0, half // p_tile, tile, 0)

    chunks = 2 * heads
    events = sorted(
        ((c // 2 + k, c, k) for c in range(chunks) for k in range(1, chips))
    )
    done = [0]
    sent = set()
    ready = []

    def send_own(c):
        start_own(c)
        sent.add(c)

    def relay_upto(rank):
        while done[0] < len(events):
            key, c, k = events[done[0]]
            if key > rank or c not in sent:
                return
            relay(c, k)
            done[0] += 1
            if k == chips - 1:
                ready.append(c)

    for h in range(min(2, heads)):
        send_head(h)
    for h in range(heads):
        def load(i, carry):
            pltpu.make_async_copy(
                w_hbm.at[pl.ds(pl.multiple_of((i * heads + h) * HD, HD), HD), :],
                wv.at[h, pl.ds(pl.multiple_of(i * HD, HD), HD), :],
                w_sem.at[h],
            ).start()
            return carry

        lax.fori_loop(0, places, load, 0)

    for step in range(heads + 1):
        h = step - 1
        if step < heads:
            for t in range(2):
                whole_wait(kvb.at[t, step], a_recv.at[step, t])
                x_copy(step, t).start()
            if step + 2 < heads:
                send_head(step + 2)
        if h >= 0:
            whole_wait(qb.at[h], a_recv.at[h, 2])
            for t in range(2):
                y_copy(h, t).wait_recv()
            attend(h, 0, tiles // 2)
            send_own(2 * h)
        if step < heads:
            for t in range(2):
                x_copy(step, t).wait_recv()
                y_copy(step, t).start()
        if h >= heads - 2:
            relay_upto(1 if h == heads - 2 else 3)
        if h >= 0:
            attend(h, tiles // 2, tiles)
            send_own(2 * h + 1)
        if h == heads - 2:
            relay_upto(2)
    while done[0] < len(events):
        key = events[done[0]][0]
        if key == events[-1][0]:
            key, c, k = events[done[0]]
            relay(c, k)
            done[0] += 1
            ready.append(c)
        else:
            relay_upto(key)
        while ready:
            project(ready.pop(0))

    for h in range(heads):
        for t in range(3):
            part = landing(t, h).at[pl.ds(0, (places - 1) * tok), :]
            whole_wait(part, a_send.at[h, t])
        for t in range(2):
            x_copy(h, t).wait_send()
            y_copy(h, t).wait_send()
    for c in range(chunks):
        for cond, copy in own_copies(c):
            if cond is None:
                copy.wait_send()
            else:
                pl.when(cond)(copy.wait_send)
        for k in range(1, chips):
            for cond, make in relay_copies(c, k):
                @pl.when(cond)
                def _():
                    make().wait_send()


def solution(mesh):
    frames = mesh.shape["tm"]
    places = mesh.shape["space"]

    def body(queries, key_vectors, value_vectors, out_weight, frame_mask):
        tok, width = queries.shape
        heads = width // HD // places
        rows = tok * places
        chips = places // 2
        cols = out_weight.shape[1]
        bf16 = jnp.bfloat16
        anyspace = pl.BlockSpec(memory_space=pl.ANY)
        dma = pltpu.SemaphoreType.DMA
        return pl.pallas_call(
            functools.partial(kernel, frames, places, heads),
            out_shape=jax.ShapeDtypeStruct((rows, cols), bf16),
            in_specs=[anyspace] * 4 + [pl.BlockSpec(memory_space=pltpu.SMEM)],
            out_specs=pl.BlockSpec(memory_space=pltpu.VMEM),
            scratch_shapes=[
                pltpu.VMEM((heads, rows, HD), bf16),
                pltpu.VMEM((2, heads, rows, HD), bf16),
                pltpu.VMEM((2, heads, rows, HD), bf16),
                pltpu.VMEM((2, heads, rows, HD), bf16),
                pltpu.VMEM((heads, rows, places * HD), bf16),
                pltpu.VMEM((heads, places * HD, cols), bf16),
                pltpu.VMEM((rows, cols), jnp.float32),
                dma((heads, 3)), dma((heads, 3)),
                dma((heads, 2)), dma((heads, 2)),
                dma((heads, 2)), dma((heads, 2)),
                dma((2 * heads, 3 + 4 * (chips - 1))),
                dma((2 * heads, 2, chips - 1)),
                dma((2 * heads, chips)),
                dma((heads,)),
            ],
            compiler_params=pltpu.CompilerParams(
                collective_id=0, has_side_effects=True,
                vmem_limit_bytes=60 * 1024 * 1024,
            ),
        )(queries, key_vectors, value_vectors, out_weight, frame_mask)

    in_specs = (
        P(("tm", "space"), None),
        P(("tm", "space"), None),
        P(("tm", "space"), None),
        P(None, "space"),
        P(),
    )
    return jax.shard_map(
        body, mesh=mesh, in_specs=in_specs, out_specs=P("tm", "space"), check_vma=False
    )
```

profile of v0, /device:TPU:0, one launch (start us, length us, event | category | flops | bytes accessed | tf_op | source)
XLA Modules:
  0.0 151.6 jit_solution(14826500163046942545)
XLA Ops:
  0.0 148.9 %shard_map.55 = bf16[1024,768]{1,0:T(8,128)(2,1)} custom-call(bf16[128,4096]{1,0:T(8,128)(2,1)} %q_hbm.1, bf16[128,4096]{1,0:T(8,128)(2,1)} %k_hbm.1, bf16[128,4096]{1,0:T(8,128)(2,1)} %v_hbm.1, bf16[4096,768]{1,0:T(8,128)(2,1)} %w_hbm.1, s32[4,4]{1,0:T(4,128)} %mask_ref.1), custom_call_target="tpu_custom_call" | custom-call | tf_op jit(solution)/shard_map/pallas_call | solution.py:305
  148.9 2.7 %copy.7 = bf16[1024,768]{1,0:T(8,128)(2,1)} copy(bf16[1024,768]{1,0:T(8,128)(2,1)} %shard_map.55) | data formatting | bytes 3145728
where the time goes:
time: 152 us
  Pallas kernels  149 us (98%)
  local copies, waits for them, and re-layouts  2.65 us (2%)
    pallas_call x1, Pallas kernels, body(): pl.pallas_call(functools.partial(kernel, frames, places, heads), out_shap...  149 us

commit v1 on v0

v1 whole, which is shorter than its diff:
```python
import functools
import math

import jax
import jax.numpy as jnp
from jax import lax
from jax.experimental import pallas as pl
from jax.experimental.pallas import tpu as pltpu
from jax.sharding import PartitionSpec as P

HD = 128
MESH = pl.DeviceIdType.MESH
WINDOW = 2
START = 6.5
STEP = 5.8
LATE = 5.8
HALF = 5.6
HOP = 1.8
TILE = 1.6
IN_HOP = 8.0
OUT_HOP = 8.0
IN_BASE = 84.0
IN_RATE = 1.6
OUT_BASE = 72.0
OUT_RATE = 2.2
KEEP = 2
EARLY = 1.0
RELAY_HOP = 4.0
PROJ = 1.0
SPREAD = 1.8
LAND = 2.0
FINAL = 95.0


def kernel(
    frames, places, heads, pieces,
    q_hbm, k_hbm, v_hbm, w_hbm, mask_ref, out_ref,
    qb, kvb, kvx, kvy, gat, wv, acc,
    a_send, a_recv, x_send, x_recv, y_send, y_recv,
    g_send, m_send, g_recv, p_recv, w_sem,
):
    f = lax.axis_index("tm")
    s = lax.axis_index("space")
    tok = q_hbm.shape[0]
    rows = tok * places
    piece = rows // pieces
    chips = places // 2
    chunks = heads * pieces
    z = lax.div(s, 2)
    core = lax.rem(s, 2)
    odd = lax.rem(f, 2)
    partner = f + 1 - 2 * odd
    onward = lax.rem(f + 2 - 4 * odd + frames, frames)
    behind = lax.rem(f - 2 + 4 * odd + frames, frames)
    far = lax.rem(f - 1 + 2 * odd + frames, frames)
    mate = 2 * z + 1 - core

    def remote(src, dst, send, recv, tm_to, space_to):
        return pltpu.make_async_remote_copy(
            src_ref=src, dst_ref=dst, send_sem=send, recv_sem=recv,
            device_id=(tm_to, space_to), device_id_type=MESH,
        )

    def whole_wait(ref, sem):
        pltpu.make_async_copy(ref, ref, sem).wait()

    barrier = pltpu.get_barrier_semaphore()
    for j in range(1, places):
        pl.semaphore_signal(
            barrier, inc=1, device_id=(f, lax.rem(s + j, places)), device_id_type=MESH
        )
    for other in (partner, onward, behind):
        pl.semaphore_signal(barrier, inc=1, device_id=(other, s), device_id_type=MESH)

    def landing(t, h):
        return qb.at[h] if t == 2 else kvb.at[t, h]

    sources = (k_hbm, v_hbm, q_hbm)
    own_rows = pl.ds(pl.multiple_of(s * tok, tok), tok)

    def head_cols(place, h):
        return pl.ds(pl.multiple_of((place * heads + h) * HD, HD), HD)

    for h in range(heads):
        for t in range(3):
            pltpu.make_async_copy(
                sources[t].at[:, head_cols(s, h)], landing(t, h).at[own_rows, :], a_recv.at[h, t]
            ).start()

    for h in range(heads):
        def load(i, carry):
            pltpu.make_async_copy(
                w_hbm.at[pl.ds(pl.multiple_of((i * heads + h) * HD, HD), HD), :],
                wv.at[h, pl.ds(pl.multiple_of(i * HD, HD), HD), :],
                w_sem.at[h],
            ).start()
            return carry

        lax.fori_loop(0, places, load, 0)

    pl.semaphore_wait(barrier, places - 1 + 3)

    items = [(0, 0), (0, 1)]
    for h in range(1, heads):
        if h < heads - 1 or heads < 3:
            items += [(h, 0), (h - 1, 2), (h, 1)]
        else:
            items += [(h, 0), (h, 1), (h - 1, 2)]
    items.append((heads - 1, 2))
    at_end = (z == 0) | (z == chips - 1)
    lower = 2 * z < chips - 1

    def send_item(i, some=None):
        h, t = items[i]
        for j in range(1, places):
            to = lax.rem(s + j, places)
            away = lax.div(to, 2)
            copy = remote(
                sources[t].at[:, head_cols(to, h)], landing(t, h).at[own_rows, :],
                a_send.at[h, t], a_recv.at[h, t], f, to,
            )
            held = at_end | ((away != z) & ((away < z) == lower))
            if some is None:
                copy.start()
            else:
                pl.when(held if some else jnp.logical_not(held))(copy.start)

    for i in range(len(items)):
        send_item(i, None if i < WINDOW else False)

    def feed(i):
        if i < len(items):
            send_item(i, True)

    def x_copy(h, t):
        return remote(
            kvb.at[t, h], kvx.at[t, h], x_send.at[h, t], x_recv.at[h, t], partner, s
        )

    def y_copy(h, t):
        return remote(
            kvx.at[t, h], kvy.at[t, h], y_send.at[h, t], y_recv.at[h, t], onward, s
        )

    def item_lands(i):
        h, t = items[i]
        whole_wait(landing(t, h), a_recv.at[h, t])
        if t < 2:
            x_copy(h, t).start()
        feed(i + WINDOW)

    def pass_on(h, t):
        x_copy(h, t).wait_recv()
        y_copy(h, t).start()

    def part(c, place):
        return gat.at[c // pieces, place, pl.ds(pl.multiple_of(c % pieces * piece, piece), piece), :]

    def hop(c, origin, slot, to_chip):
        p = part(c, 2 * origin + core)
        return remote(p, p, g_send.at[c, slot], g_recv.at[c, origin], f, 2 * to_chip + core)

    def to_mate(c, origin):
        p = part(c, 2 * origin + core)
        return remote(p, p, m_send.at[c, origin], p_recv.at[c, origin], f, mate)

    def from_mate(c, origin):
        p = part(c, 2 * origin + 1 - core)
        return remote(p, p, m_send.at[c, origin], p_recv.at[c, origin], f, mate)

    def own_hops(c):
        return [(z < chips - 1, hop(c, z, 0, z + 1)), (z > 0, hop(c, z, 1, z - 1))]

    def far_hops(c):
        if chips < 3:
            return []
        return [(z == 0, hop(c, z, 2, z + 2)), (z == chips - 1, hop(c, z, 3, z - 2))]

    def send_own(c):
        for cond, copy in own_hops(c):
            pl.when(cond)(copy.start)
        to_mate(c, z).start()

    def send_far(c):
        for cond, copy in far_hops(c):
            pl.when(cond)(copy.start)

    def passes_on(k, up):
        if up:
            on = (z >= k) & (z < chips - 1)
            return on & (z != 1) if k == 1 else on
        on = (z + k <= chips - 1) & (z > 0)
        return on & (z != chips - 2) if k == 1 else on

    def relay(c, k, edge, more):
        for up in (True, False):
            origin = z - k if up else z + k
            slot = 4 + 2 * (k - 1) + (0 if up else 1)
            here = z >= k if up else z + k <= chips - 1
            here &= (z == k if edge else z != k) if up else (
                z + k == chips - 1 if edge else z + k != chips - 1)
            if k < chips - 1:
                on = passes_on(k, up)
                here &= on if more else jnp.logical_not(on)

            @pl.when(here)
            def _():
                hop(c, origin, slot, z).wait_recv()

            if more:
                @pl.when(here)
                def _():
                    hop(c, origin, slot, z + 1 if up else z - 1).start()

            @pl.when(here)
            def _():
                to_mate(c, origin).start()

    stages = [
        (k, edge, k - 2 if edge and k > 1 else k - 1)
        for k in range(1, chips) for edge in (False, True)
        if edge or k < chips - 1
    ]
    near_pen = jnp.where(mask_ref[f, partner] == 1, 0.0, jnp.inf).astype(jnp.float32)
    far_pen = jnp.where(mask_ref[f, far] == 1, 0.0, jnp.inf).astype(jnp.float32)
    factor = math.log2(math.e) / math.sqrt(HD)

    def attend(h, i):
        at = pl.ds(pl.multiple_of(i * piece, piece), piece)
        q = qb[h, at, :]
        places_kv = ((kvb, None), (kvx, near_pen), (kvy, far_pen))
        scores = []
        top = None
        for ref, pen in places_kv:
            sc = lax.dot_general(
                q, ref[0, h], (((1,), (1,)), ((), ())),
                preferred_element_type=jnp.float32,
            )
            scores.append(sc)
            best = jnp.max(sc, axis=1, keepdims=True)
            best = best if pen is None else best - pen
            top = best if top is None else jnp.maximum(top, best)
        total = None
        mixed = None
        for sc, (ref, pen) in zip(scores, places_kv):
            level = top if pen is None else top + pen
            e = jnp.exp2((sc - level) * factor)
            summed = jnp.sum(e, axis=1, keepdims=True)
            prod = jnp.dot(
                e.astype(jnp.bfloat16), ref[1, h], preferred_element_type=jnp.float32
            )
            total = summed if total is None else total + summed
            mixed = prod if mixed is None else mixed + prod
        gat[h, s, at, :] = (mixed / total).astype(jnp.bfloat16)

    def project(c):
        h = c // pieces
        for o in range(chips):
            from_mate(c, o).wait_recv()
        at = pl.ds(pl.multiple_of(c % pieces * piece, piece), piece)
        a = jnp.concatenate([gat[h, p, at, :] for p in range(places)], axis=1)
        prod = acc[at, :] + jnp.dot(a, wv[h], preferred_element_type=jnp.float32)

        @pl.when(h < heads - 1)
        def _():
            acc[at, :] = prod

        @pl.when(h == heads - 1)
        def _():
            out_ref[at, :] = prod.astype(out_ref.dtype)

    def loop(first, last, fn):
        def step(i, carry):
            fn(i)
            return carry

        if last > first:
            lax.fori_loop(first, last, step, 0)

    acc[...] = jnp.zeros_like(acc)
    scope = jax.named_scope
    events = []
    landed = {}
    x_free = y_free = 0.0
    for i, (h, t) in enumerate(items):
        landed[h, t] = START + STEP * (i + 1) if i < 6 else START + 6 * STEP + LATE * (i - 5)
        events.append((landed[h, t], f"item{i}", functools.partial(item_lands, i)))
        if t < 2:
            x_free = max(x_free, landed[h, t]) + HALF
            events.append((x_free + HOP, f"x{h}{t}", functools.partial(pass_on, h, t)))
            y_free = max(y_free, x_free + HOP) + HALF
            landed[h, t] = y_free + HOP
    now = 0.0
    tile_at = []
    for c in range(chunks):
        now = max([now] + [landed[c // pieces, t] for t in range(3)])
        tile_at.append(now)
        now += TILE
    ends = [0.0] * chunks
    kept = max(heads - KEEP, 0) * pieces
    if kept:
        flush_at = max(tile_at[kept - 1] + TILE, tile_at[kept] - EARLY)
        events.append((flush_at, "flush", lambda: loop(0, kept, send_far)))
    inner_at, outer_at = IN_BASE, OUT_BASE
    for c in range(chunks):
        inner_at = max(inner_at + IN_RATE, tile_at[c] + TILE + IN_HOP)
        outer_at = max(outer_at + OUT_RATE, tile_at[c] + TILE + OUT_HOP)
        for k, edge, depth in stages:
            at = (outer_at if edge else inner_at) + RELAY_HOP * depth
            for more in (True, False):
                if more and k == chips - 1:
                    continue
                when = at if more else max(at + LAND, FINAL + 1.4 * c)
                events.append((when, f"r{k}{int(edge)}{int(more)}_{c}", functools.partial(relay, c, k, edge, more)))
                ends[c] = max(ends[c], when)
    events.sort(key=lambda e: e[0])

    def run(when, fn):
        groups = []
        for c in range(chunks):
            group = []
            while events and events[0][0] <= when[c]:
                group.append(events.pop(0)[1:])
            groups.append(group)

        def step(c):
            for j, group in enumerate(groups):
                if group:
                    @pl.when(c == j)
                    def _():
                        for name, event in group:
                            with scope(name):
                                event()
            fn(c)

        loop(0, chunks, step)

    def tile(c):
        h = c // pieces

        @pl.when(c % pieces == 0)
        def _():
            with scope("ready"):
                for t in range(2):
                    y_copy(h, t).wait_recv()
        with scope("attend"):
            attend(h, c % pieces)
            send_own(c)
            pl.when(c >= kept)(lambda: send_far(c))

    def last(c):
        with scope("project"):
            project(c)

    run(tile_at, tile)
    for h in range(heads):
        whole_wait(wv.at[h], w_sem.at[h])
    run([max(e + PROJ, tile_at[-1] + SPREAD * c) for c, e in enumerate(ends[:-1])] + [math.inf], last)

    for h in range(heads):
        for t in range(3):
            sent = landing(t, h).at[pl.ds(0, (places - 1) * tok), :]
            whole_wait(sent, a_send.at[h, t])
        for t in range(2):
            x_copy(h, t).wait_send()
            y_copy(h, t).wait_send()

    def drain(c):
        for cond, copy in own_hops(c) + far_hops(c):
            pl.when(cond)(copy.wait_send)
        for o in range(chips):
            to_mate(c, o).wait_send()
        for k in range(1, chips - 1):
            for up in (True, False):
                slot = 4 + 2 * (k - 1) + (0 if up else 1)
                origin = z - k if up else z + k

                @pl.when(passes_on(k, up))
                def _():
                    hop(c, origin, slot, z + 1 if up else z - 1).wait_send()

    loop(0, chunks, drain)


def solution(mesh):
    frames = mesh.shape["tm"]
    places = mesh.shape["space"]

    def body(queries, key_vectors, value_vectors, out_weight, frame_mask):
        tok, width = queries.shape
        heads = width // HD // places
        rows = tok * places
        chips = places // 2
        cols = out_weight.shape[1]
        pieces = max(1, rows // 256)
        chunks = heads * pieces
        bf16 = jnp.bfloat16
        anyspace = pl.BlockSpec(memory_space=pl.ANY)
        dma = pltpu.SemaphoreType.DMA
        return pl.pallas_call(
            functools.partial(kernel, frames, places, heads, pieces),
            out_shape=jax.ShapeDtypeStruct((rows, cols), bf16),
            in_specs=[anyspace] * 4 + [pl.BlockSpec(memory_space=pltpu.SMEM)],
            out_specs=pl.BlockSpec(memory_space=pltpu.VMEM),
            scratch_shapes=[
                pltpu.VMEM((heads, rows, HD), bf16),
                pltpu.VMEM((2, heads, rows, HD), bf16),
                pltpu.VMEM((2, heads, rows, HD), bf16),
                pltpu.VMEM((2, heads, rows, HD), bf16),
                pltpu.VMEM((heads, places, rows, HD), bf16),
                pltpu.VMEM((heads, places * HD, cols), bf16),
                pltpu.VMEM((rows, cols), jnp.float32),
                dma((heads, 3)), dma((heads, 3)),
                dma((heads, 2)), dma((heads, 2)),
                dma((heads, 2)), dma((heads, 2)),
                dma((chunks, 4 + 2 * (chips - 1))),
                dma((chunks, chips)),
                dma((chunks, chips)),
                dma((chunks, chips)),
                dma((heads,)),
            ],
            compiler_params=pltpu.CompilerParams(
                collective_id=0, has_side_effects=True,
                vmem_limit_bytes=60 * 1024 * 1024,
            ),
        )(queries, key_vectors, value_vectors, out_weight, frame_mask)

    in_specs = (
        P(("tm", "space"), None),
        P(("tm", "space"), None),
        P(("tm", "space"), None),
        P(None, "space"),
        P(),
    )
    return jax.shard_map(
        body, mesh=mesh, in_specs=in_specs, out_specs=P("tm", "space"), check_vma=False
    )
```

time: 152 us -> 146 us (0.961)
  Pallas kernels: 149 us -> 143 us
    pallas_call x1, Pallas kernels: 149 us -> 143 us  [body(): pl.pallas_call(functools.partial(kernel, frames, places, heads, pieces),...]
where the time goes in v1:
time: 146 us; the launch traced here: 145 us
  Pallas kernels  143 us (98%)
  local copies, waits for them, and re-layouts  2.65 us (2%)
    pallas_call x1, Pallas kernels, body(): pl.pallas_call(functools.partial(kernel, frames, places, heads, pieces),...  143 us

profile of v1, /device:TPU:0, one launch (start us, length us, event | category | flops | bytes accessed | tf_op | source)
XLA Modules:
  0.0 145.3 jit_solution(4127199640044663697)
XLA Ops:
  0.0 142.7 %shard_map.55 = bf16[1024,768]{1,0:T(8,128)(2,1)} custom-call(bf16[128,4096]{1,0:T(8,128)(2,1)} %q_hbm.1, bf16[128,4096]{1,0:T(8,128)(2,1)} %k_hbm.1, bf16[128,4096]{1,0:T(8,128)(2,1)} %v_hbm.1, bf16[4096,768]{1,0:T(8,128)(2,1)} %w_hbm.1, s32[4,4]{1,0:T(4,128)} %mask_ref.1), custom_call_target="tpu_custom_call" | custom-call | tf_op jit(solution)/shard_map/pallas_call | solution.py:400
  142.7 2.7 %copy.7 = bf16[1024,768]{1,0:T(8,128)(2,1)} copy(bf16[1024,768]{1,0:T(8,128)(2,1)} %shard_map.55) | data formatting | bytes 3145728

commit v2 on v1

--- a/solution.py
+++ b/solution.py
@@ -11,6 +11,7 @@
 HD = 128
 MESH = pl.DeviceIdType.MESH
 WINDOW = 2
+WINDOW_OUT = 6
 START = 6.5
 STEP = 5.8
 LATE = 5.8
@@ -27,6 +28,7 @@
 EARLY = 1.0
 RELAY_HOP = 4.0
 PROJ = 1.0
+DRAIN = 4
 SPREAD = 1.8
 LAND = 2.0
 FINAL = 95.0
@@ -110,7 +112,7 @@
     at_end = (z == 0) | (z == chips - 1)
     lower = 2 * z < chips - 1
 
-    def send_item(i, some=None):
+    def send_item(i, kinds):
         h, t = items[i]
         for j in range(1, places):
             to = lax.rem(s + j, places)
@@ -119,18 +121,21 @@
                 sources[t].at[:, head_cols(to, h)], landing(t, h).at[own_rows, :],
                 a_send.at[h, t], a_recv.at[h, t], f, to,
             )
-            held = at_end | ((away != z) & ((away < z) == lower))
-            if some is None:
+            outward = (away != z) & ((away < z) == lower)
+            masks = (jnp.logical_not(at_end | outward), at_end, jnp.logical_not(at_end) & outward)
+            go = [m for m, wanted in zip(masks, kinds) if wanted]
+            if len(go) == len(masks):
                 copy.start()
-            else:
-                pl.when(held if some else jnp.logical_not(held))(copy.start)
+            elif go:
+                pl.when(functools.reduce(jnp.logical_or, go))(copy.start)
 
     for i in range(len(items)):
-        send_item(i, None if i < WINDOW else False)
+        send_item(i, (True, i < WINDOW, i < WINDOW_OUT))
 
     def feed(i):
-        if i < len(items):
-            send_item(i, True)
+        for j, kinds in ((i + WINDOW, (False, True, False)), (i + WINDOW_OUT, (False, False, True))):
+            if j < len(items):
+                send_item(j, kinds)
 
     def x_copy(h, t):
         return remote(
@@ -147,7 +152,7 @@
         whole_wait(landing(t, h), a_recv.at[h, t])
         if t < 2:
             x_copy(h, t).start()
-        feed(i + WINDOW)
+        feed(i)
 
     def pass_on(h, t):
         x_copy(h, t).wait_recv()
@@ -276,6 +281,20 @@
 
         if last > first:
             lax.fori_loop(first, last, step, 0)
+
+    def drain(c):
+        for cond, copy in own_hops(c) + far_hops(c):
+            pl.when(cond)(copy.wait_send)
+        for o in range(chips):
+            to_mate(c, o).wait_send()
+        for k in range(1, chips - 1):
+            for up in (True, False):
+                slot = 4 + 2 * (k - 1) + (0 if up else 1)
+                origin = z - k if up else z + k
+
+                @pl.when(passes_on(k, up))
+                def _():
+                    hop(c, origin, slot, z + 1 if up else z - 1).wait_send()
 
     acc[...] = jnp.zeros_like(acc)
     scope = jax.named_scope
@@ -351,12 +370,9 @@
     def last(c):
         with scope("project"):
             project(c)
+        pl.when(c >= DRAIN)(lambda: drain(c - DRAIN))
 
     run(tile_at, tile)
-    for h in range(heads):
-        whole_wait(wv.at[h], w_sem.at[h])
-    run([max(e + PROJ, tile_at[-1] + SPREAD * c) for c, e in enumerate(ends[:-1])] + [math.inf], last)
-
     for h in range(heads):
         for t in range(3):
             sent = landing(t, h).at[pl.ds(0, (places - 1) * tok), :]
@@ -364,22 +380,11 @@
         for t in range(2):
             x_copy(h, t).wait_send()
             y_copy(h, t).wait_send()
-
-    def drain(c):
-        for cond, copy in own_hops(c) + far_hops(c):
-            pl.when(cond)(copy.wait_send)
-        for o in range(chips):
-            to_mate(c, o).wait_send()
-        for k in range(1, chips - 1):
-            for up in (True, False):
-                slot = 4 + 2 * (k - 1) + (0 if up else 1)
-                origin = z - k if up else z + k
-
-                @pl.when(passes_on(k, up))
-                def _():
-                    hop(c, origin, slot, z + 1 if up else z - 1).wait_send()
-
-    loop(0, chunks, drain)
+    for h in range(heads):
+        whole_wait(wv.at[h], w_sem.at[h])
+    run([max(e + PROJ, tile_at[-1] + SPREAD * c) for c, e in enumerate(ends[:-1])] + [math.inf], last)
+
+    loop(max(chunks - DRAIN, 0), chunks, drain)
 
 
 def solution(mesh):
@@ -399,7 +404,7 @@
         dma = pltpu.SemaphoreType.DMA
         return pl.pallas_call(
             functools.partial(kernel, frames, places, heads, pieces),
-            out_shape=jax.ShapeDtypeStruct((rows, cols), bf16),
+            out_shape=pltpu.VMEM((rows, cols), bf16),
             in_specs=[anyspace] * 4 + [pl.BlockSpec(memory_space=pltpu.SMEM)],
             out_specs=pl.BlockSpec(memory_space=pltpu.VMEM),
             scratch_shapes=[

time: 146 us -> 142 us (0.973)
  Pallas kernels: 143 us -> 141 us
  local copies, waits for them, and re-layouts: 2.65 us -> 1.15 us
    pallas_call x1, Pallas kernels: 143 us -> 141 us  [body(): pl.pallas_call(functools.partial(kernel, frames, places, heads, pieces),...]
    unnamed x1, local copies, waits for them, and re-layouts: 2.65 us -> 1.15 us
where the time goes in v2:
time: 142 us
  Pallas kernels  141 us (99%)
    pallas_call x1, Pallas kernels, body(): pl.pallas_call(functools.partial(kernel, frames, places, heads, pieces),...  141 us

profile of v2, /device:TPU:0, one launch (start us, length us, event | category | flops | bytes accessed | tf_op | source)
XLA Modules:
  0.0 142.1 jit_solution(15285431439585805466)
XLA Ops:
  0.0 141.0 %shard_map.55 = bf16[1024,768]{1,0:T(8,128)(2,1)S(1)} custom-call(bf16[128,4096]{1,0:T(8,128)(2,1)} %q_hbm.1, bf16[128,4096]{1,0:T(8,128)(2,1)} %k_hbm.1, bf16[128,4096]{1,0:T(8,128)(2,1)} %v_hbm.1, bf16[4096,768]{1,0:T(8,128)(2,1)} %w_hbm.1, s32[4,4]{1,0:T(4,128)} %mask_ref.1), custom_call_target="tpu_custom_call" | custom-call | tf_op jit(solution)/shard_map/pallas_call | solution.py:405
  141.0 1.1 copy.7

commit v3 on v2

--- a/solution.py
+++ b/solution.py
@@ -11,10 +11,11 @@
 HD = 128
 MESH = pl.DeviceIdType.MESH
 WINDOW = 2
-WINDOW_OUT = 6
+WINDOW_OUT = 3
 START = 6.5
 STEP = 5.8
 LATE = 5.8
+LAST = 4.0
 HALF = 5.6
 HOP = 1.8
 TILE = 1.6
@@ -22,7 +23,7 @@
 OUT_HOP = 8.0
 IN_BASE = 84.0
 IN_RATE = 1.6
-OUT_BASE = 72.0
+OUT_BASE = 74.0
 OUT_RATE = 2.2
 KEEP = 2
 EARLY = 1.0
@@ -31,7 +32,7 @@
 DRAIN = 4
 SPREAD = 1.8
 LAND = 2.0
-FINAL = 95.0
+FINAL = 88.0
 
 
 def kernel(
@@ -303,6 +304,8 @@
     x_free = y_free = 0.0
     for i, (h, t) in enumerate(items):
         landed[h, t] = START + STEP * (i + 1) if i < 6 else START + 6 * STEP + LATE * (i - 5)
+        if i == len(items) - 1:
+            landed[h, t] += LAST
         events.append((landed[h, t], f"item{i}", functools.partial(item_lands, i)))
         if t < 2:
             x_free = max(x_free, landed[h, t]) + HALF

time: 142 us -> 141 us (level)
  no operation moved by 1% of the time
where the time goes in v3:
time: 141 us
  Pallas kernels  140 us (99%)
    pallas_call x1, Pallas kernels, body(): pl.pallas_call(functools.partial(kernel, frames, places, heads, pieces),...  140 us

profile of v3, /device:TPU:0, one launch (start us, length us, event | category | flops | bytes accessed | tf_op | source)
XLA Modules:
  0.0 141.3 jit_solution(14649312338650217469)
XLA Ops:
  0.0 140.1 %shard_map.55 = bf16[1024,768]{1,0:T(8,128)(2,1)S(1)} custom-call(bf16[128,4096]{1,0:T(8,128)(2,1)} %q_hbm.1, bf16[128,4096]{1,0:T(8,128)(2,1)} %k_hbm.1, bf16[128,4096]{1,0:T(8,128)(2,1)} %v_hbm.1, bf16[4096,768]{1,0:T(8,128)(2,1)} %w_hbm.1, s32[4,4]{1,0:T(4,128)} %mask_ref.1), custom_call_target="tpu_custom_call" | custom-call | tf_op jit(solution)/shard_map/pallas_call | solution.py:408
  140.1 1.1 copy.7
